TPU v7x, 32 devices: a whole 2x2x4 slice. The times are simulated.
32 devices in a mesh: gx: 4 (over y, core), gy: 4 (over z), gz: 2 (over x).
Axes of the slice: x: 2, y: 2, z: 4, core: 2. Of those that a mesh axis runs over, the one named last changes fastest.
Arguments:
- grads: bfloat16 [32, 4, 1, 8, 3584], P(('gx', 'gy', 'gz')), may hold values from -1196032 to 1196032
- counts: int32 [32], P(('gx', 'gy', 'gz')), may hold values from 1 to 4
- total_tokens: int32 [1], replicated, may hold values from 4000000 to 15999999
- master: float32 [1, 8, 3584], P(None, 'gy', ('gx', 'gz')), may hold values from -6 to 6
- moment1: float32 [1, 8, 3584], P(None, 'gy', ('gx', 'gz')), may hold values from -2 to 2
- moment2: float32 [1, 8, 3584], P(None, 'gy', ('gx', 'gz')), may hold values from 0.01 to 1
Outputs:
- params: bfloat16 [1, 8, 3584], replicated
- master_out: float32 [1, 8, 3584], P(None, 'gy', ('gx', 'gz'))
- moment1_out: float32 [1, 8, 3584], P(None, 'gy', ('gx', 'gz'))
- moment2_out: float32 [1, 8, 3584], P(None, 'gy', ('gx', 'gz'))
All inputs are finite; a program needn't handle non-finite values.
Results may differ from a plain program's by a relative error of at most 0.0004.
Values may be sent and summed in bfloat16 or wider, within the bound.
A program may use at most 64 MiB of HBM per device.

v0:
```python
import jax
import jax.numpy as jnp
from jax import lax
from jax.sharding import PartitionSpec as P


def body(grads, counts, total_tokens, master, moment1, moment2):
    rank_grads = grads[0]
    slots = jnp.arange(rank_grads.shape[0], dtype=jnp.int32)
    weights = (slots < counts[0]).astype(jnp.float32)
    accumulated = jnp.zeros(rank_grads.shape[1:], jnp.float32)
    for slot in range(rank_grads.shape[0]):
        accumulated = accumulated + weights[slot] * rank_grads[slot].astype(jnp.float32)
    partial_value = lax.psum_scatter(accumulated, ("gx", "gz"), scatter_dimension=2, tiled=True)
    summed = lax.psum_scatter(partial_value, "gy", scatter_dimension=1, tiled=True)
    gradient = summed / total_tokens.astype(jnp.float32)[0]
    moment1_out = 0.9 * moment1 + 0.1 * gradient
    moment2_out = 0.95 * moment2 + 0.05 * gradient * gradient
    first_fix = 1.0 - 0.9**10
    second_fix = 1.0 - 0.95**10
    update = moment1_out / first_fix / (jnp.sqrt(moment2_out / second_fix) + 1e-08)
    master_out = master - 0.01 * (update + 0.1 * master)
    shard_params = master_out.astype(jnp.bfloat16)
    wide_params = lax.all_gather(shard_params, ("gx", "gz"), axis=2, tiled=True)
    params = lax.all_gather(wide_params, "gy", axis=1, tiled=True)
    return (params, master_out, moment1_out, moment2_out)


def solution(mesh):
    return jax.shard_map(
        body,
        mesh=mesh,
        in_specs=(
            P(("gx", "gy", "gz"), None, None, None, None),
            P(("gx", "gy", "gz")),
            P(),
            P(None, "gy", ("gx", "gz")),
            P(None, "gy", ("gx", "gz")),
            P(None, "gy", ("gx", "gz")),
        ),
        out_specs=(
            P(),
            P(None, "gy", ("gx", "gz")),
            P(None, "gy", ("gx", "gz")),
            P(None, "gy", ("gx", "gz")),
        ),
        check_vma=False,
    )
```

profile of v0, /device:TPU:0, one launch (start us, length us, event | category | flops | bytes accessed | tf_op | source)
XLA Modules:
  0.0 125.8 jit_solution(12063351168490614243)
XLA Ops:
  7.2 0.0 reduce-scatter.5.cloned.1.call-start
  7.9 0.6 fusion.3
  8.5 3.5 %add_bitcast_fusion = f32[1,8,3584]{2,1,0:T(8,128)S(1)} fusion(bf16[1,4,1,8,3584]{4,3,2,1,0:T(8,128)(2,1)} %param.6, f32[]{:T(128)} %bitcast.8, f32[]{:T(128)} %bitcast.7, f32[]{:T(128)} %bitcast.6, f32[]{:T(128)} %bitcast.5), kind=kLoop, calls=%fused_computation | loop fusion | flops 315392 | bytes 344080 | tf_op jit(solution)/shard_map/add | solution.py:13
  12.0 0.0 copy-start.3
  12.0 0.0 copy-start
  12.0 0.0 copy-start.1
  12.0 0.0 copy-start.2
  12.0 3.0 %copy.13 = f32[1,8,3584]{1,0,2:T(1,128)} copy(f32[1,8,3584]{2,1,0:T(8,128)S(1)} %add_bitcast_fusion) | data formatting | bytes 229376
  15.0 0.0 reduce-scatter.5.cloned.1.call-update
  15.7 0.0 copy-done.3
  15.7 0.6 dynamic-slice
  17.0 40.5 %reduce-scatter.5.cloned.1.call-done = f32[448,8]{1,0:T(8,128)} async-done(((f32[3584,8]{1,0:T(8,128)}), f32[448,8]{1,0:T(8,128)}) %reduce-scatter.5.cloned.1.call-update) | async-done | bytes 14352
  57.5 1.0 copy.14
  58.5 18.7 %all-reduce = f32[1,8,448]{2,1,0:T(8,128)S(1)} all-reduce(f32[1,8,448]{2,1,0:T(8,128)S(1)} %copy.14), channel_id=3, replica_groups=mesh['gx'=4,'gy'=4,'gz'=2] {'gy'}, use_global_device_ids=true, to_apply=%region_1.0.clone | all-reduce | flops 3584 | bytes 28672
  77.2 0.0 copy-done
  77.2 0.0 copy-done.1
  77.2 0.0 copy-done.2
  77.3 0.6 fusion.1
  77.9 0.2 copy.10
  78.1 24.8 %all_gather.6 = bf16[1,2,3584]{1,0,2:T(2,128)(2,1)S(1)} all-gather(bf16[1,2,448]{1,0,2:T(2,128)(2,1)S(1)} %copy.10), channel_id=1, replica_groups=mesh['gx'=4,'gy'=4,'gz'=2] {'gx','gz'}, dimensions={2}, use_global_device_ids=true | all-gather | bytes 16128 | tf_op jit(solution)/shard_map/all_gather | solution.py:24
  102.9 2.0 %copy.11 = bf16[1,2,3584]{2,0,1:T(2,128)(2,1)S(1)} copy(bf16[1,2,3584]{1,0,2:T(2,128)(2,1)S(1)} %all_gather.6) | data formatting | bytes 28672 | tf_op jit(solution)/shard_map/all_gather | solution.py:24
  104.9 13.4 %all_gather.7 = bf16[1,8,3584]{2,0,1:T(2,128)(2,1)S(1)} all-gather(bf16[1,2,3584]{2,0,1:T(2,128)(2,1)S(1)} %copy.11), channel_id=1, replica_groups=mesh['gx'=4,'gy'=4,'gz'=2] {'gy'}, dimensions={1}, use_global_device_ids=true | all-gather | bytes 71680 | tf_op jit(solution)/shard_map/all_gather | solution.py:25
  118.3 0.6 copy.12
  (1 shorter events, 0.0 us)
Async XLA Ops:
  7.2 50.3 %reduce-scatter.5.cloned.1.call-start = ((), (), s32[]{:S(2)}) async-start(), calls=%async_computation.1 | async-start | bytes 2064384
  12.0 3.7 %copy-start.3 = (u32[32]{0:T(128)S(1)}, u32[32]{0:T(128)}, u32[]{:S(2)}) copy-start(u32[32]{0:T(128)} %constant.25) | copy-start | bytes 388
  12.0 65.2 %copy-start = (f32[1,2,448]{2,1,0:T(2,128)S(1)}, f32[1,2,448]{2,1,0:T(2,128)}, u32[]{:S(2)}) copy-start(f32[1,2,448]{2,1,0:T(2,128)} %param.9) | copy-start | bytes 10756
  12.0 65.2 %copy-start.1 = (f32[1,2,448]{2,1,0:T(2,128)S(1)}, f32[1,2,448]{2,1,0:T(2,128)}, u32[]{:S(2)}) copy-start(f32[1,2,448]{2,1,0:T(2,128)} %param.10) | copy-start | bytes 10756
  12.0 65.2 %copy-start.2 = (f32[1,2,448]{2,1,0:T(2,128)S(1)}, f32[1,2,448]{2,1,0:T(2,128)}, u32[]{:S(2)}) copy-start(f32[1,2,448]{2,1,0:T(2,128)} %param.11) | copy-start | bytes 10756
Sparse Core Ops, SparseCore 0:
  15.2 42.2 reduce-scatter.4
where the time goes:
time: 126 us
  blocking collectives  57 us (45%)
  waiting for transfers between devices  40.5 us (32%)
  between operations  16.1 us (13%)
  local copies, waits for them, and re-layouts  8.05 us (6%)
  other arithmetic  4.17 us (3%)
    unnamed x2, waiting for transfers between devices  40.5 us
    all_gather x1, blocking collectives, body(): wide_params = lax.all_gather(shard_params, ('gx', 'gz'), axis=2, tiled=True)  24.8 us
    unnamed x1, blocking collectives  18.7 us
    all_gather x1, blocking collectives, body(): params = lax.all_gather(wide_params, 'gy', axis=1, tiled=True)  13.4 us
    unnamed x12, local copies, waits for them, and re-layouts  5.27 us
    add x1, other arithmetic, body(): accumulated + weights[slot] * rank_grads[slot].astype(jnp.float32)  3.53 us
  transfers between devices with their start and end apart: 1, of which 1 were waited for; matrix products, arithmetic and copies ran while one was open for 0% of the time, Pallas kernels for 0%

commit v1 on v0

--- a/solution.py
+++ b/solution.py
@@ -22,7 +22,12 @@
     master_out = master - 0.01 * (update + 0.1 * master)
     shard_params = master_out.astype(jnp.bfloat16)
     wide_params = lax.all_gather(shard_params, ("gx", "gz"), axis=2, tiled=True)
-    params = lax.all_gather(wide_params, "gy", axis=1, tiled=True)
+    ring = [wide_params]
+    for hop in range(3):
+        ring.append(lax.ppermute(ring[-1], "gy", [(dev, (dev + 1) % 4) for dev in range(4)]))
+    params = jnp.roll(
+        jnp.concatenate(ring[::-1], axis=1), (lax.axis_index("gy") + 1) * ring[0].shape[1], axis=1
+    )
     return (params, master_out, moment1_out, moment2_out)
 
 

time: 126 us -> 129 us (1.024)
  waiting for transfers between devices: 40.5 us -> 57.1 us
  blocking collectives: 57 us -> 43.6 us
    ppermute x0 -> x3, waiting for transfers between devices: none -> 16.5 us  [body(): lax.ppermute(ring[-1], 'gy', [(dev, (dev + 1) % 4) for dev in range(4)])]
    all_gather x1 -> x0, blocking collectives: 13.4 us -> none  [body(): params = lax.all_gather(wide_params, 'gy', axis=1, tiled=True)]
    unnamed x12 -> x11, local copies, waits for them, and re-layouts: 5.27 us -> 4.63 us
  transfers between devices with their start and end apart: 1 -> 4, of which waited for: 1 -> 4; matrix products, arithmetic and copies ran while one was open for 0% -> 0% of each run, Pallas kernels for 0% -> 0%
where the time goes in v1:
time: 129 us
  waiting for transfers between devices  57.1 us (44%)
  blocking collectives  43.6 us (34%)
  between operations  16.1 us (12%)
  local copies, waits for them, and re-layouts  8 us (6%)
  other arithmetic  4.17 us (3%)
    unnamed x2, waiting for transfers between devices  40.5 us
    all_gather x1, blocking collectives, body(): wide_params = lax.all_gather(shard_params, ('gx', 'gz'), axis=2, tiled=True)  24.8 us
    unnamed x1, blocking collectives  18.7 us
    ppermute x3, waiting for transfers between devices, body(): lax.ppermute(ring[-1], 'gy', [(dev, (dev + 1) % 4) for dev in range(4)])  16.5 us
    unnamed x11, local copies, waits for them, and re-layouts  4.63 us
    add x1, other arithmetic, body(): accumulated + weights[slot] * rank_grads[slot].astype(jnp.float32)  3.53 us
  transfers between devices with their start and end apart: 4, of which 4 were waited for; matrix products, arithmetic and copies ran while one was open for 0% of the time, Pallas kernels for 0%

profile of v1, /device:TPU:0, one launch (start us, length us, event | category | flops | bytes accessed | tf_op | source)
XLA Modules:
  0.0 129.0 jit_solution(9101140034016788427)
XLA Ops:
  7.2 0.0 reduce-scatter.5.cloned.1.call-start
  7.9 0.6 fusion.3
  8.5 3.5 %add_bitcast_fusion = f32[1,8,3584]{2,1,0:T(8,128)S(1)} fusion(bf16[1,4,1,8,3584]{4,3,2,1,0:T(8,128)(2,1)} %param.6, f32[]{:T(128)} %bitcast.8, f32[]{:T(128)} %bitcast.7, f32[]{:T(128)} %bitcast.6, f32[]{:T(128)} %bitcast.5), kind=kLoop, calls=%fused_computation | loop fusion | flops 315392 | bytes 344080 | tf_op jit(solution)/shard_map/add | solution.py:13
  12.0 0.0 copy-start.3
  12.0 0.0 copy-start
  12.0 0.0 copy-start.1
  12.0 0.0 copy-start.2
  12.0 3.0 %copy.16 = f32[1,8,3584]{1,0,2:T(1,128)} copy(f32[1,8,3584]{2,1,0:T(8,128)S(1)} %add_bitcast_fusion) | data formatting | bytes 229376
  15.0 0.0 reduce-scatter.5.cloned.1.call-update
  15.7 0.0 copy-done.3
  15.7 0.6 dynamic-slice
  17.0 40.5 %reduce-scatter.5.cloned.1.call-done = f32[448,8]{1,0:T(8,128)} async-done(((f32[3584,8]{1,0:T(8,128)}), f32[448,8]{1,0:T(8,128)}) %reduce-scatter.5.cloned.1.call-update) | async-done | bytes 14352
  57.5 1.0 copy.17
  58.5 18.7 %all-reduce = f32[1,8,448]{2,1,0:T(8,128)S(1)} all-reduce(f32[1,8,448]{2,1,0:T(8,128)S(1)} %copy.17), channel_id=3, replica_groups=mesh['gx'=4,'gy'=4,'gz'=2] {'gy'}, use_global_device_ids=true, to_apply=%region_1.0.clone | all-reduce | flops 3584 | bytes 28672
  77.2 0.0 copy-done
  77.2 0.0 copy-done.1
  77.2 0.0 copy-done.2
  77.2 0.6 fusion.1
  77.9 0.2 copy.12
  78.1 24.8 %all_gather.3 = bf16[1,2,3584]{1,0,2:T(2,128)(2,1)S(1)} all-gather(bf16[1,2,448]{1,0,2:T(2,128)(2,1)S(1)} %copy.12), channel_id=1, replica_groups=mesh['gx'=4,'gy'=4,'gz'=2] {'gx','gz'}, dimensions={2}, use_global_device_ids=true | all-gather | bytes 16128 | tf_op jit(solution)/shard_map/all_gather | solution.py:24
  102.9 1.8 %copy.13 = bf16[1,2,3584]{2,1,0:T(2,128)(2,1)S(1)} copy(bf16[1,2,3584]{1,0,2:T(2,128)(2,1)S(1)} %all_gather.3) | data formatting | bytes 28672 | tf_op jit(solution)/shard_map/all_gather | solution.py:24
  104.7 0.1 collective-permute-start
  104.8 5.5 %collective-permute-done = bf16[1,2,3584]{2,1,0:T(2,128)(2,1)S(1)} collective-permute-done((bf16[1,2,3584]{2,1,0:T(2,128)(2,1)S(1)}, bf16[1,2,3584]{2,1,0:T(2,128)(2,1)S(1)}, u32[]{:S(2)}, u32[]{:S(2)}) %collective-permute-start) | collective-permute-done | bytes 14368 | tf_op jit(solution)/shard_map/ppermute | solution.py:27
  110.3 0.0 collective-permute-start.1
  110.3 5.5 %collective-permute-done.1 = bf16[1,2,3584]{2,1,0:T(2,128)(2,1)S(1)} collective-permute-done((bf16[1,2,3584]{2,1,0:T(2,128)(2,1)S(1)}, bf16[1,2,3584]{2,1,0:T(2,128)(2,1)S(1)}, u32[]{:S(2)}, u32[]{:S(2)}) %collective-permute-start.1) | collective-permute-done | bytes 14368 | tf_op jit(solution)/shard_map/ppermute | solution.py:27
  115.8 0.0 collective-permute-start.2
  115.8 5.5 %collective-permute-done.2 = bf16[1,2,3584]{2,1,0:T(2,128)(2,1)S(1)} collective-permute-done((bf16[1,2,3584]{2,1,0:T(2,128)(2,1)S(1)}, bf16[1,2,3584]{2,1,0:T(2,128)(2,1)S(1)}, u32[]{:S(2)}, u32[]{:S(2)}) %collective-permute-start.2) | collective-permute-done | bytes 14368 | tf_op jit(solution)/shard_map/ppermute | solution.py:27
  121.3 0.2 concatenate.6
  121.5 0.7 constant_dynamic-slice_fusion
  (1 shorter events, 0.0 us)
Async XLA Ops:
  7.2 50.3 %reduce-scatter.5.cloned.1.call-start = ((), (), s32[]{:S(2)}) async-start(), calls=%async_computation.1 | async-start | bytes 2064384
  12.0 3.7 %copy-start.3 = (u32[32]{0:T(128)S(1)}, u32[32]{0:T(128)}, u32[]{:S(2)}) copy-start(u32[32]{0:T(128)} %constant.57) | copy-start | bytes 388
  12.0 65.2 %copy-start = (f32[1,2,448]{2,1,0:T(2,128)S(1)}, f32[1,2,448]{2,1,0:T(2,128)}, u32[]{:S(2)}) copy-start(f32[1,2,448]{2,1,0:T(2,128)} %param.9) | copy-start | bytes 10756
  12.0 65.2 %copy-start.1 = (f32[1,2,448]{2,1,0:T(2,128)S(1)}, f32[1,2,448]{2,1,0:T(2,128)}, u32[]{:S(2)}) copy-start(f32[1,2,448]{2,1,0:T(2,128)} %param.10) | copy-start | bytes 10756
  12.0 65.2 %copy-start.2 = (f32[1,2,448]{2,1,0:T(2,128)S(1)}, f32[1,2,448]{2,1,0:T(2,128)}, u32[]{:S(2)}) copy-start(f32[1,2,448]{2,1,0:T(2,128)} %param.11) | copy-start | bytes 10756
  104.7 5.6 %collective-permute-start = (bf16[1,2,3584]{2,1,0:T(2,128)(2,1)S(1)}, bf16[1,2,3584]{2,1,0:T(2,128)(2,1)S(1)}, u32[]{:S(2)}, u32[]{:S(2)}) collective-permute-start(bf16[1,2,3584]{2,1,0:T(2,128)(2,1)S(1)} %copy.13), channel_id=1, source_target_pairs={{0,2},{2,4},{4,6},{6,0},{1,3},{3,5},{5,7},{7,1},{8,10},{10,12},{12... | collective-permute-start | bytes 43016 | tf_op jit(solution)/shard_map/ppermute | solution.py:27
  110.3 5.5 %collective-permute-start.1 = (bf16[1,2,3584]{2,1,0:T(2,128)(2,1)S(1)}, bf16[1,2,3584]{2,1,0:T(2,128)(2,1)S(1)}, u32[]{:S(2)}, u32[]{:S(2)}) collective-permute-start(bf16[1,2,3584]{2,1,0:T(2,128)(2,1)S(1)} %collective-permute-done), channel_id=1, source_target_pairs={{0,2},{2,4},{4,6},{6,0},{1,3},{3,5},{5,7},{7,1},{8,10},{10,12},{12... | collective-permute-start | bytes 43016 | tf_op jit(solution)/shard_map/ppermute | solution.py:27
  115.8 5.5 %collective-permute-start.2 = (bf16[1,2,3584]{2,1,0:T(2,128)(2,1)S(1)}, bf16[1,2,3584]{2,1,0:T(2,128)(2,1)S(1)}, u32[]{:S(2)}, u32[]{:S(2)}) collective-permute-start(bf16[1,2,3584]{2,1,0:T(2,128)(2,1)S(1)} %collective-permute-done.1), channel_id=1, source_target_pairs={{0,2},{2,4},{4,6},{6,0},{1,3},{3,5},{5,7},{7,1},{8,10},{10,12},{12... | collective-permute-start | bytes 43016 | tf_op jit(solution)/shard_map/ppermute | solution.py:27
Sparse Core Ops, SparseCore 0:
  15.2 42.2 reduce-scatter.4
